TPU v7x, 32 devices: a whole 2x2x4 slice. The times are simulated.
32 devices in a mesh: gx: 4 (over z), gy: 2 (over y), gz: 4 (over x, core).
Axes of the slice: x: 2, y: 2, z: 4, core: 2. Of those that a mesh axis runs over, the one named last changes fastest.
Arguments:
- coords: float32 [3, 65536], P(None, ('gx', 'gy', 'gz')), may hold values from 0 to 3
- anchor: float32 [3, 65536], P(None, ('gx', 'gy', 'gz')), may hold values from -73 to 76
- atom_types: int32 [65536], P(('gx', 'gy', 'gz')), may hold values from 0 to 63
- halo_send: int32 [27904], P(('gx', 'gy', 'gz')), may hold values from 0 to 2047, as said below
- neighbours: int32 [8192, 8], P(('gx', 'gy', 'gz')), may hold values from 0 to 364, as said below
- live_counts: int32 [8192], P(('gx', 'gy', 'gz')), may hold values from 1 to 8
- rep_coef: float32 [64], replicated, may hold values from 0.5 to 2
- disp_coef: float32 [64], replicated, may hold values from 0.2 to 1
- charge: float32 [64], replicated, may hold values from -1 to 1
- step_history: float32 [8, 3, 65536], P(None, None, ('gx', 'gy', 'gz')), may hold values from -9 to 9
- grad_history: float32 [8, 3, 65536], P(None, None, ('gx', 'gy', 'gz')), may hold values from -72 to 72, as said below
Outputs:
- new_coords: float32 [3, 65536], P(None, ('gx', 'gy', 'gz'))
- energy: float32 [], replicated
Inputs may be any that keep to these rules, and one draw needn't show every extreme that they name: `halo_send`: each of a domain's seven blocks holds distinct local atom indices, rising. `neighbours`: slot 0 of row r is r mod 256, the row's own cluster. `grad_history`: the product of each entry with the matching step_history entry is not negative, and each pair's inner product is positive.
All inputs are finite; a program needn't handle non-finite values.
Results may differ from a plain program's by a relative error of at most 0.0003.
Values sent between devices are 32-bit elements; how exact they have to be, the bound alone decides.
No kernel may reach another device: no remote copies, remote signals or barrier semaphores. Data moves between devices by JAX's collectives and lax.ppermute only.
A program may use at most 64 MiB of HBM per device.

v0:
```python
import math

import jax
import jax.numpy as jnp
from jax import lax
from jax.sharding import PartitionSpec as P

domain_side = 3.0
step_length = 0.5
axis_bits = {"gx": 4, "gy": 2, "gz": 1}
axis_component = {"gx": 0, "gy": 1, "gz": 2}


def shifted(value, axis, steps):
    count = lax.axis_size(axis)
    pairs = [(source, (source + steps) % count) for source in range(count)]
    return lax.ppermute(value, axis, pairs)


def export_sizes(atoms_local):
    face_rows = atoms_local // 8
    edge_rows = max(atoms_local // 64, 8)
    corner_rows = max(atoms_local // 512, 8)
    return [face_rows, face_rows, edge_rows, face_rows, edge_rows, edge_rows, corner_rows]


def tile_gradient(ext_pos, ext_par, neighbours, live_counts):
    highest = lax.Precision.HIGHEST
    ext_clusters = ext_pos.shape[1] // 8
    pos_tiles = ext_pos.reshape(3, ext_clusters, 8).transpose(0, 2, 1)
    par_tiles = ext_par.reshape(3, ext_clusters, 8).transpose(0, 2, 1)
    both_tiles = jnp.concatenate([pos_tiles, par_tiles], axis=0)
    cluster_rows = neighbours.shape[0]
    list_width = neighbours.shape[1]
    block_rows = math.gcd(256, cluster_rows)
    block_count = cluster_rows // block_rows
    atom_rank = jnp.arange(8, dtype=jnp.int32)
    ordered_pair = (atom_rank[:, None] < atom_rank[None, :]).astype(jnp.float32)[:, :, None]
    slot_rank = jnp.tile(jnp.arange(list_width, dtype=jnp.int32), block_rows)
    ext_ids = jnp.arange(ext_clusters, dtype=jnp.int32)

    def one_block(state_pair, block_id):
        gradient, energy = state_pair
        first_row = block_id * block_rows
        listed = neighbours.reshape(-1)
        selector = (listed[:, None] == ext_ids[None, :]).astype(jnp.float32)
        live_count = jnp.repeat(live_counts, list_width)
        home_ids = jnp.repeat(first_row + jnp.arange(block_rows, dtype=jnp.int32), list_width)
        live_mask = (slot_rank < live_count).astype(jnp.float32)
        weight = live_mask[None, None, :] * jnp.where(
            (listed == home_ids)[None, None, :], ordered_pair, 1.0
        )
        pos_home = jnp.repeat(
            lax.dynamic_slice_in_dim(pos_tiles, first_row, block_rows, 2), list_width, axis=2
        )
        par_home = jnp.repeat(
            lax.dynamic_slice_in_dim(par_tiles, first_row, block_rows, 2), list_width, axis=2
        )
        other_tiles = jnp.einsum("caj,kj->cak", both_tiles, selector, precision=highest)
        pos_other = other_tiles[:3]
        par_other = other_tiles[3:]
        offset = pos_home[:, :, None, :] - pos_other[:, None, :, :]
        dist_sq = jnp.sum(offset * offset, axis=0)
        inverse = 1.0 / (1.0 + dist_sq)
        repulse = par_home[0][:, None, :] * par_other[0][None, :, :]
        attract = par_home[1][:, None, :] * par_other[1][None, :, :]
        coulomb = par_home[2][:, None, :] * par_other[2][None, :, :]
        root_inv = jnp.sqrt(inverse)
        pair_energy = repulse * inverse * inverse - attract * inverse + coulomb * root_inv
        slope = 2.0 * repulse * inverse - attract + 0.5 * coulomb / root_inv
        factor = -2.0 * weight * slope * inverse * inverse
        push_term = factor[None] * offset
        home_grad = jnp.sum(push_term, axis=2).reshape(3, 8, block_rows, list_width).sum(axis=3)
        other_grad = -jnp.sum(push_term, axis=1)
        gradient = gradient + jnp.einsum("cak,kj->caj", other_grad, selector, precision=highest)
        current = lax.dynamic_slice_in_dim(gradient, first_row, block_rows, 2)
        gradient = lax.dynamic_update_slice_in_dim(gradient, current + home_grad, first_row, 2)
        energy = energy + jnp.sum(weight * pair_energy)
        return ((gradient, energy), None)

    initial = (jnp.zeros((3, 8, ext_clusters), jnp.float32), jnp.zeros((), jnp.float32))
    (gradient, energy), unused = lax.scan(
        one_block, initial, jnp.arange(block_count, dtype=jnp.int32)
    )
    return (gradient.transpose(0, 2, 1).reshape(3, -1), energy)


def pass_along(payload, axis_name, offset):
    if axis_name == "gx":
        return shifted(payload, "gx", offset)
    if axis_name == "gy":
        return shifted(payload, "gy", offset)
    return shifted(payload, "gz", offset)


def two_loop(cross_products, grad_dots):
    memory = cross_products.shape[0] // 2
    basis_size = 2 * memory + 1
    gram_full = jnp.zeros((basis_size, basis_size), jnp.float32)
    gram_full = (
        gram_full.at[0, 1:].set(grad_dots).at[1:, 0].set(grad_dots).at[1:, 1:].set(cross_products)
    )
    unit_rows = jnp.eye(basis_size, dtype=jnp.float32)
    inverse_sy = [1.0 / cross_products[hist_id, memory + hist_id] for hist_id in range(memory)]
    alphas = [None] * memory
    coeffs = unit_rows[0]
    for hist_id in reversed(range(memory)):
        alphas[hist_id] = inverse_sy[hist_id] * jnp.sum(gram_full[1 + hist_id] * coeffs)
        coeffs = coeffs - alphas[hist_id] * unit_rows[1 + memory + hist_id]
    scaling = (
        cross_products[memory - 1, 2 * memory - 1] / cross_products[2 * memory - 1, 2 * memory - 1]
    )
    coeffs = scaling * coeffs
    for hist_id in range(memory):
        beta_term = inverse_sy[hist_id] * jnp.sum(gram_full[1 + memory + hist_id] * coeffs)
        coeffs = coeffs + (alphas[hist_id] - beta_term) * unit_rows[1 + hist_id]
    return coeffs


def on_device(
    coords,
    anchor,
    atom_types,
    halo_send,
    neighbours,
    live_counts,
    rep_coef,
    disp_coef,
    charge,
    step_history,
    grad_history,
):
    highest = lax.Precision.HIGHEST
    atoms_local = coords.shape[1]
    size_list = export_sizes(atoms_local)
    start_list = [sum(size_list[:block_pos]) for block_pos in range(7)]
    history = jnp.concatenate([step_history, grad_history], axis=0).reshape(
        2 * step_history.shape[0], -1
    )
    type_table = jnp.stack([rep_coef, disp_coef, charge])
    type_ids = jnp.arange(type_table.shape[1], dtype=jnp.int32)
    one_hot = (atom_types[None, :] == type_ids[:, None]).astype(jnp.float32)
    params = jnp.dot(type_table, one_hot, precision=highest)
    local_rows = jnp.concatenate([coords, params], axis=0)
    exported = jnp.take(local_rows, halo_send, axis=1)
    axis_order = ["gz", "gy", "gx"]
    held_blocks = {}
    for block_code in range(1, 8):
        block_start = start_list[block_code - 1]
        held_blocks[block_code] = exported[:, block_start : block_start + size_list[block_code - 1]]
    for axis_name in axis_order:
        bit_value = axis_bits[axis_name]
        movers = [block_code for block_code in range(1, 8) if block_code & bit_value]
        payload = jnp.concatenate([held_blocks[block_code] for block_code in movers], axis=1)
        arrived = pass_along(payload, axis_name, -1)
        moved_by = jnp.array(
            [
                domain_side if component == axis_component[axis_name] else 0.0
                for component in range(6)
            ],
            jnp.float32,
        )
        arrived = arrived + moved_by[:, None]
        cursor = 0
        for block_code in movers:
            held_blocks[block_code] = arrived[:, cursor : cursor + size_list[block_code - 1]]
            cursor = cursor + size_list[block_code - 1]
    halo_part = jnp.concatenate([held_blocks[block_code] for block_code in range(1, 8)], axis=1)
    extended = jnp.concatenate([local_rows, halo_part], axis=1)
    gradient_ext, energy_local = tile_gradient(extended[:3], extended[3:], neighbours, live_counts)
    gradient = gradient_ext[:, :atoms_local]
    back_blocks = {}
    for block_code in range(1, 8):
        begin = atoms_local + start_list[block_code - 1]
        back_blocks[block_code] = gradient_ext[:, begin : begin + size_list[block_code - 1]]
    for axis_name in reversed(axis_order):
        bit_value = axis_bits[axis_name]
        movers = [block_code for block_code in range(1, 8) if block_code & bit_value]
        payload = jnp.concatenate([back_blocks[block_code] for block_code in movers], axis=1)
        arrived = pass_along(payload, axis_name, 1)
        cursor = 0
        for block_code in movers:
            back_blocks[block_code] = arrived[:, cursor : cursor + size_list[block_code - 1]]
            cursor = cursor + size_list[block_code - 1]
    returned = jnp.concatenate([back_blocks[block_code] for block_code in range(1, 8)], axis=1)
    gradient = gradient.at[:, halo_send].add(returned)
    displacement = coords - anchor
    gradient = gradient + displacement
    energy_local = energy_local + 0.5 * jnp.sum(displacement * displacement)
    flat_grad = gradient.reshape(-1)
    grad_dots_local = jnp.dot(history, flat_grad, precision=highest)
    cross_products, grad_dots, energy_sum = lax.psum(
        (jnp.dot(history, history.T, precision=highest), grad_dots_local, energy_local),
        ("gx", "gy", "gz"),
    )
    coeffs = two_loop(cross_products, grad_dots)
    basis_rows = jnp.concatenate([flat_grad[None], history], axis=0)
    direction = jnp.dot(coeffs, basis_rows, precision=highest).reshape(3, atoms_local)
    new_coords = coords - step_length * direction
    atoms_total = atoms_local * lax.axis_size("gx") * lax.axis_size("gy") * lax.axis_size("gz")
    return (new_coords, energy_sum / atoms_total)


def solution(mesh):
    placed = (
        P(None, ("gx", "gy", "gz")),
        P(None, ("gx", "gy", "gz")),
        P(("gx", "gy", "gz")),
        P(("gx", "gy", "gz")),
        P(("gx", "gy", "gz"), None),
        P(("gx", "gy", "gz")),
        P(),
        P(),
        P(),
        P(None, None, ("gx", "gy", "gz")),
        P(None, None, ("gx", "gy", "gz")),
    )
    return jax.shard_map(
        on_device,
        mesh=mesh,
        in_specs=placed,
        out_specs=(P(None, ("gx", "gy", "gz")), P()),
        check_vma=False,
    )
```

profile of v0, /device:TPU:0, one launch (start us, length us, event | category | flops | bytes accessed | tf_op | source)
XLA Modules:
  0.0 138.2 jit_solution(14454354531783564797)
XLA Ops:
  0.7 0.7 compare_select_fusion
  1.4 0.7 compare_and_fusion
  2.1 1.0 fusion.20
  3.1 0.8 pad_maximum_fusion
  4.3 1.9 %gather_fusion = f32[872,6]{1,0:T(8,128)S(1)} fusion(f32[6,2048]{0,1:T(8,128)S(1)} %copy.62, s32[1024]{0:T(1024)S(1)} %pad_clamp_fusion), kind=kCustom, calls=%fused_computation | custom fusion | bytes 45344 | tf_op jit(solution)/shard_map/jit(_take)/gather | solution.py:145
  6.7 2.4 %collective-permute-start = (f32[6,328]{1,0:T(8,128)S(1)}, f32[6,328]{1,0:T(8,128)S(1)}, u32[]{:S(2)}, u32[]{:S(2)}) collective-permute-start(f32[6,328]{1,0:T(8,128)S(1)} %pad_maximum_fusion.1), channel_id=1, source_target_pairs={{0,3},{1,0},{2,1},{3,2},{4,7},{5,4},{6,5},{7,6},{8,11},{9,8},{10,9... | collective-permute-start | bytes 23624 | tf_op jit(solution)/shard_map/ppermute | solution.py:17
  9.3 1.2 collective-permute-done
  10.8 1.5 %collective-permute-start.1 = (f32[6,328]{1,0:T(8,128)S(1)}, f32[6,328]{1,0:T(8,128)S(1)}, u32[]{:S(2)}, u32[]{:S(2)}) collective-permute-start(f32[6,328]{1,0:T(8,128)S(1)} %pad_maximum_fusion.2), channel_id=1, source_target_pairs={{0,4},{4,0},{1,5},{5,1},{2,6},{6,2},{3,7},{7,3},{8,12},{12,8},{9,1... | collective-permute-start | bytes 23624 | tf_op jit(solution)/shard_map/ppermute | solution.py:17
  12.4 1.2 convolution_bitcast_fusion
  13.6 0.9 collective-permute-done.1
  14.8 3.6 %collective-permute-start.2 = (f32[6,328]{1,0:T(8,128)S(1)}, f32[6,328]{1,0:T(8,128)S(1)}, u32[]{:S(2)}, u32[]{:S(2)}) collective-permute-start(f32[6,328]{1,0:T(8,128)S(1)} %pad_maximum_fusion.3), channel_id=1, source_target_pairs={{0,24},{8,0},{16,8},{24,16},{1,25},{9,1},{17,9},{25,17},{2,26},{10... | collective-permute-start | bytes 23624 | tf_op jit(solution)/shard_map/ppermute | solution.py:17
  21.1 1.2 fusion.3
  22.3 0.7 slice.459
  23.0 0.7 slice_bitcast_fusion.7
  23.6 0.8 slice_bitcast_fusion.1
  24.4 0.7 copy.67
  25.1 1.6 %broadcast_in_dim.99 = f32[3,8,256,8]{3,2,1,0:T(8,128)S(1)} broadcast(f32[3,8,256]{2,1,0:T(8,128)} %copy.67), dimensions={0,1,2} | broadcast | bytes 221184 | tf_op jit(solution)/shard_map/while/body/eval_jaxpr/broadcast_in_dim | solution.py:53
  26.7 2.8 %sub.111 = f32[3,8,2048]{2,1,0:T(8,128)} reshape(f32[3,8,256,8]{3,2,1,0:T(8,128)S(1)} %broadcast_in_dim.99) | data formatting | bytes 393216 | tf_op jit(solution)/shard_map/while/body/eval_jaxpr/sub | solution.py:62
  29.5 1.1 slice_bitcast_fusion.4
  33.6 1.0 fusion.18
  34.6 1.3 fusion.5
  35.9 2.7 %reshape.266 = f32[3,8,256,8]{3,2,1,0:T(8,128)S(1)} reshape(f32[3,8,2048]{2,1,0:T(8,128)} %get-tuple-element.71) | data formatting | bytes 393216 | tf_op jit(solution)/shard_map/while/body/eval_jaxpr/reshape | solution.py:73
  38.6 3.0 %fusion.1 = f32[3,8,365]{2,1,0:T(8,128)} fusion(s32[2048]{0:T(1024)S(1)} %copy-done.10, f32[3,8,2048]{2,1,0:T(8,128)} %get-tuple-element.72), kind=kOutput, calls=%fused_computation.4 | convolution fusion | flops 216082432 | bytes 239840 | tf_op jit(solution)/shard_map/while/body/eval_jaxpr/cak,kj->caj/dot_general | solution.py:75
  41.5 1.5 %reduce_sum.206 = f32[3,8,256]{2,1,0:T(8,128)} reduce(f32[3,8,256,8]{3,2,1,0:T(8,128)S(1)} %reshape.266, f32[]{:T(128)} %constant.140.clone.1), dimensions={3}, to_apply=%region_4.5 | reduce | flops 43008 | bytes 221188 | tf_op jit(solution)/shard_map/while/body/eval_jaxpr/reduce_sum | solution.py:73
  43.0 1.4 fusion.28
  44.4 1.0 copy.70
  46.2 5.4 %collective-permute-done.3 = f32[3,328]{1,0:T(4,128)S(1)} collective-permute-done((f32[3,328]{1,0:T(4,128)S(1)}, f32[3,328]{1,0:T(4,128)S(1)}, u32[]{:S(2)}, u32[]{:S(2)}) %collective-permute-start.3) | collective-permute-done | bytes 3968 | tf_op jit(solution)/shard_map/ppermute | solution.py:17
  51.8 1.5 %collective-permute-start.4 = (f32[3,328]{1,0:T(4,128)S(1)}, f32[3,328]{1,0:T(4,128)S(1)}, u32[]{:S(2)}, u32[]{:S(2)}) collective-permute-start(f32[3,328]{1,0:T(4,128)S(1)} %pad_maximum_fusion.4), channel_id=1, source_target_pairs={{0,4},{4,0},{1,5},{5,1},{2,6},{6,2},{3,7},{7,3},{8,12},{12,8},{9,1... | collective-permute-start | bytes 11816 | tf_op jit(solution)/shard_map/ppermute | solution.py:17
  53.3 0.7 fusion.90
  54.0 1.4 %collective-permute-done.4 = f32[3,328]{1,0:T(4,128)S(1)} collective-permute-done((f32[3,328]{1,0:T(4,128)S(1)}, f32[3,328]{1,0:T(4,128)S(1)}, u32[]{:S(2)}, u32[]{:S(2)}) %collective-permute-start.4) | collective-permute-done | bytes 3968 | tf_op jit(solution)/shard_map/ppermute | solution.py:17
  58.0 0.7 collective-permute-done.5
  59.2 6.4 %scatter_fusion = f32[3,2048]{0,1:T(8,128)S(1)} fusion(f32[3,2048]{0,1:T(8,128)S(1)} %copy.71, s32[872]{0:T(1024)S(1)} %compare_select_fusion, f32[872,3]{1,0:T(8,128)S(1)} %copy.72), kind=kCustom, calls=%fused_computation.1 | custom fusion | flops 2616 | bytes 34880 | tf_op jit(solution)/shard_map/scatter-add | solution.py:186
  66.9 37.5 %all-reduce = (f32[16,16]{1,0:T(8,128)S(1)}, f32[16]{0:T(128)S(1)}, f32[]{:T(128)}) all-reduce(f32[16,16]{1,0:T(8,128)S(1)} %copy-done.8, f32[16]{0:T(128)S(1)} %convolution_bitcast_fusion.1, f32[]{:T(128)S(6)} %add.171), channel_id=1, replica_groups=mesh['gx'=4,'gy'=2,'gz'=4] {'gx','gy','gz'}, use_global_device_ids=true, to_apply=%region_0.1 | all-reduce | flops 273 | bytes 2184 | tf_op jit(solution)/shard_map/psum | solution.py:192
  104.4 0.7 fusion.87
  105.1 1.6 %scatter.10 = f32[17,17]{1,0:T(8,128)S(1)} dynamic-update-slice(f32[17,17]{1,0:T(8,128)S(1)} %broadcast_in_dim.88, f32[1,16]{1,0:T(1,128)S(1)} %bitcast.102, s32[]{:T(128)} %bitcast.23, s32[]{:T(128)} %bitcast.24) | dynamic-update-slice | bytes 132 | tf_op jit(solution)/shard_map/scatter | solution.py:101
  107.0 0.8 scatter.14
  110.9 0.7 fusion.66
  113.6 0.6 fusion.64
  114.9 0.7 fusion.62
  118.6 0.7 fusion.58
  122.5 0.7 fusion.54
  124.5 0.7 fusion.52
  127.0 0.7 fusion.48
  128.3 0.7 fusion.46
  129.6 0.7 fusion.44
  131.0 0.6 fusion.42
  135.2 0.6 fusion.10
  135.8 0.6 fusion.27
  (120 shorter events, 15.4 us)
Async XLA Ops:
  0.6 8.5 %copy-start.6 = (f32[8,3,2048]{2,0,1:T(8,128)S(1)}, f32[8,3,2048]{2,0,1:T(8,128)}, u32[]{:S(2)}) copy-start(f32[8,3,2048]{2,0,1:T(8,128)} %param.29) | copy-start | bytes 589828
  0.6 8.5 %copy-start.7 = (f32[8,3,2048]{2,0,1:T(8,128)S(1)}, f32[8,3,2048]{2,0,1:T(8,128)}, u32[]{:S(2)}) copy-start(f32[8,3,2048]{2,0,1:T(8,128)} %param.30) | copy-start | bytes 589828
  0.7 8.5 %copy-start.14 = (s32[256]{0:T(256)S(1)}, s32[256]{0:T(256)}, u32[]{:S(2)}) copy-start(s32[256]{0:T(256)} %param.25) | copy-start | bytes 3076
  3.1 7.4 %copy-start.17 = (f32[6]{0:T(128)S(1)}, f32[6]{0:T(128)}, u32[]{:S(2)}) copy-start(f32[6]{0:T(128)} %constant.151.clone) | copy-start | bytes 76
  4.3 10.3 %copy-start.16 = (f32[6]{0:T(128)S(1)}, f32[6]{0:T(128)}, u32[]{:S(2)}) copy-start(f32[6]{0:T(128)} %constant.152.clone) | copy-start | bytes 76
  4.3 14.1 %copy-start.13 = (s32[256,8]{0,1:T(8,128)S(1)}, s32[256,8]{0,1:T(8,128)}, u32[]{:S(2)}) copy-start(s32[256,8]{0,1:T(8,128)} %param.24) | copy-start | bytes 24580
  6.2 13.6 %copy-start.15 = (f32[6]{0:T(128)S(1)}, f32[6]{0:T(128)}, u32[]{:S(2)}) copy-start(f32[6]{0:T(128)} %constant.153.clone) | copy-start | bytes 76
  6.7 3.8 %collective-permute-start = (f32[6,328]{1,0:T(8,128)S(1)}, f32[6,328]{1,0:T(8,128)S(1)}, u32[]{:S(2)}, u32[]{:S(2)}) collective-permute-start(f32[6,328]{1,0:T(8,128)S(1)} %pad_maximum_fusion.1), channel_id=1, source_target_pairs={{0,3},{1,0},{2,1},{3,2},{4,7},{5,4},{6,5},{7,6},{8,11},{9,8},{10,9... | collective-permute-start | bytes 23624 | tf_op jit(solution)/shard_map/ppermute | solution.py:17
  10.8 3.7 %collective-permute-start.1 = (f32[6,328]{1,0:T(8,128)S(1)}, f32[6,328]{1,0:T(8,128)S(1)}, u32[]{:S(2)}, u32[]{:S(2)}) collective-permute-start(f32[6,328]{1,0:T(8,128)S(1)} %pad_maximum_fusion.2), channel_id=1, source_target_pairs={{0,4},{4,0},{1,5},{5,1},{2,6},{6,2},{3,7},{7,3},{8,12},{12,8},{9,1... | collective-permute-start | bytes 23624 | tf_op jit(solution)/shard_map/ppermute | solution.py:17
  14.8 5.0 %collective-permute-start.2 = (f32[6,328]{1,0:T(8,128)S(1)}, f32[6,328]{1,0:T(8,128)S(1)}, u32[]{:S(2)}, u32[]{:S(2)}) collective-permute-start(f32[6,328]{1,0:T(8,128)S(1)} %pad_maximum_fusion.3), channel_id=1, source_target_pairs={{0,24},{8,0},{16,8},{24,16},{1,25},{9,1},{17,9},{25,17},{2,26},{10... | collective-permute-start | bytes 23624 | tf_op jit(solution)/shard_map/ppermute | solution.py:17
  18.6 2.4 %copy-start.9 = (s32[2048]{0:T(1024)}, s32[2048]{0:T(1024)S(1)}, u32[]{:S(2)}) copy-start(s32[2048]{0:T(1024)S(1)} %reshape.262) | copy-start | bytes 24580
  31.9 1.5 %copy-start = (f32[3,8,2048]{2,1,0:T(8,128)S(1)}, f32[3,8,2048]{2,1,0:T(8,128)}, u32[]{:S(2)}) copy-start(f32[3,8,2048]{2,1,0:T(8,128)} %slice.459) | copy-start | bytes 589828
  31.9 1.5 %copy-start.1 = (f32[3,8,2048]{2,1,0:T(8,128)S(1)}, f32[3,8,2048]{2,1,0:T(8,128)}, u32[]{:S(2)}) copy-start(f32[3,8,2048]{2,1,0:T(8,128)} %sub.111) | copy-start | bytes 589828
  32.5 1.1 copy-start.3
  32.5 1.1 copy-start.4
  32.5 1.1 copy-start.5
  32.5 1.1 copy-start.12
  35.9 2.7 %copy-start.10 = (s32[2048]{0:T(1024)S(1)}, s32[2048]{0:T(1024)}, u32[]{:S(2)}) copy-start(s32[2048]{0:T(1024)} %copy-done.9) | copy-start | bytes 24580
  43.0 12.6 %copy-start.2 = (f32[3,2048]{1,0:T(4,128)S(1)}, f32[3,2048]{1,0:T(4,128)}, u32[]{:S(2)}) copy-start(f32[3,2048]{1,0:T(4,128)} %param.20) | copy-start | bytes 73732
  43.0 12.6 %copy-start.11 = (f32[3,2048]{1,0:T(4,128)S(1)}, f32[3,2048]{1,0:T(4,128)}, u32[]{:S(2)}) copy-start(f32[3,2048]{1,0:T(4,128)} %param.21) | copy-start | bytes 73732
  45.8 5.9 %collective-permute-start.3 = (f32[3,328]{1,0:T(4,128)S(1)}, f32[3,328]{1,0:T(4,128)S(1)}, u32[]{:S(2)}, u32[]{:S(2)}) collective-permute-start(f32[3,328]{1,0:T(4,128)S(1)} %slice.467), channel_id=1, source_target_pairs={{0,8},{8,16},{16,24},{24,0},{1,9},{9,17},{17,25},{25,1},{2,10},{10... | collective-permute-start | bytes 11816 | tf_op jit(solution)/shard_map/ppermute | solution.py:17
  51.8 3.6 %collective-permute-start.4 = (f32[3,328]{1,0:T(4,128)S(1)}, f32[3,328]{1,0:T(4,128)S(1)}, u32[]{:S(2)}, u32[]{:S(2)}) collective-permute-start(f32[3,328]{1,0:T(4,128)S(1)} %pad_maximum_fusion.4), channel_id=1, source_target_pairs={{0,4},{4,0},{1,5},{5,1},{2,6},{6,2},{3,7},{7,3},{8,12},{12,8},{9,1... | collective-permute-start | bytes 11816 | tf_op jit(solution)/shard_map/ppermute | solution.py:17
  55.6 3.1 %collective-permute-start.5 = (f32[3,328]{1,0:T(4,128)S(1)}, f32[3,328]{1,0:T(4,128)S(1)}, u32[]{:S(2)}, u32[]{:S(2)}) collective-permute-start(f32[3,328]{1,0:T(4,128)S(1)} %pad_maximum_fusion.5), channel_id=1, source_target_pairs={{0,1},{1,2},{2,3},{3,0},{4,5},{5,6},{6,7},{7,4},{8,9},{9,10},{10,1... | collective-permute-start | bytes 11816 | tf_op jit(solution)/shard_map/ppermute | solution.py:17
  58.9 7.9 %copy-start.8 = (f32[16,16]{1,0:T(8,128)S(1)}, f32[16,16]{1,0:T(8,128)}, u32[]{:S(2)}) copy-start(f32[16,16]{1,0:T(8,128)} %convolution_bitcast_fusion) | copy-start | bytes 3076
where the time goes:
time: 140 us; the launch traced here: 138 us
  blocking collectives  37.5 us (27%)
  other arithmetic  26.8 us (19%)
  local copies, waits for them, and re-layouts  25.8 us (18%)
  between operations  20.9 us (15%)
  waiting for transfers between devices  10 us (7%)
  starting transfers between devices  9.5 us (7%)
  matrix products  7.65 us (5%)
    psum x1, blocking collectives, on_device(): lax.psum((jnp.dot(history, history.T, precision=highest), grad_dots_local...  37.5 us
    ppermute x6, waiting for transfers between devices, shifted(): return lax.ppermute(value, axis, pairs)  10 us
    ppermute x6, starting transfers between devices, shifted(): return lax.ppermute(value, axis, pairs)  9.5 us
    scatter-add x1, other arithmetic, on_device(): gradient = gradient.at[:, halo_send].add(returned)  6.44 us
    reduce_sum x8, other arithmetic, two_loop(): jnp.sum(gram_full[1 + memory + hist_id] * coeffs)  5.12 us
    reduce_sum x8, other arithmetic, two_loop(): jnp.sum(gram_full[1 + hist_id] * coeffs)  5.11 us
    dot_general x1, matrix products, one_block(): jnp.einsum('cak,kj->caj', other_grad, selector, precision=highest)  2.95 us
  transfers between devices with their start and end apart: 6, of which 6 were waited for; matrix products, arithmetic and copies ran while one was open for 3% of the time, Pallas kernels for 0%

commit v1 on v0

v1 whole, which is shorter than its diff:
```python
import functools

import jax
import jax.numpy as jnp
from jax import lax
from jax.experimental import pallas as pl
from jax.experimental.pallas import tpu as pltpu
from jax.sharding import PartitionSpec as P

domain_side = 3.0
step_length = 0.5
AXES = ("gx", "gy", "gz")
f32 = jnp.float32
bf16 = jnp.bfloat16
i32 = jnp.int32


def export_sizes(atoms_local):
    face_rows = atoms_local // 8
    edge_rows = max(atoms_local // 64, 8)
    corner_rows = max(atoms_local // 512, 8)
    return face_rows, edge_rows, corner_rows


def shifted(value, axis, steps):
    count = lax.axis_size(axis)
    pairs = [(source, (source + steps) % count) for source in range(count)]
    return lax.ppermute(value, axis, pairs)


def iota(shape, dim):
    return lax.broadcasted_iota(i32, shape, dim)


def split_parts(value, parts):
    pieces = []
    for part in range(parts):
        piece = value.astype(bf16)
        pieces.append(piece)
        if part + 1 < parts:
            value = value - piece.astype(f32)
    return pieces


def join_parts(stacked, rows, parts):
    total = stacked[(parts - 1) * rows :]
    for part in reversed(range(parts - 1)):
        total = total + stacked[part * rows : (part + 1) * rows]
    return total


def dot_nn(left, right):
    return lax.dot_general(left, right, (((1,), (0,)), ((), ())), preferred_element_type=f32)


def dot_nt(left, right):
    return lax.dot_general(left, right, (((1,), (1,)), ((), ())), preferred_element_type=f32)


def one_hot(condition):
    return jnp.where(condition, 1.0, 0.0).astype(bf16)


def slab_order(sizes):
    face, edge, corner = sizes
    return 3 * face, 3 * edge + corner


def reordered_send(send, sizes):
    face, edge, corner = sizes
    lane = iota(send.shape, 1)
    to_front = pltpu.roll(send, send.shape[1] - edge, 1)
    to_back = pltpu.roll(send, face, 1)
    moved = jnp.where(lane < 3 * face, to_front, to_back)
    return jnp.where((lane >= 2 * face) & (lane < 3 * face + edge), moved, send)


def send_one_hot(send_row, first, rows):
    row = iota((rows, send_row.shape[1]), 0) + first
    return one_hot(row == send_row)


def export_kernel(sizes, send_ref, coords_ref, types_ref, rep_ref, disp_ref, charge_ref, step_ref, diff_ref, out_ref, par_ref, data_ref):
    atoms = coords_ref.shape[1]
    ntypes = rep_ref.shape[1]
    kinds = one_hot(types_ref[...] == iota((ntypes, atoms), 0))
    sub = iota((8, ntypes), 0)
    table = jnp.where(sub == 0, rep_ref[...], jnp.where(sub == 1, disp_ref[...], jnp.where(sub == 2, charge_ref[...], 0.0)))
    table = jnp.concatenate(split_parts(table, 3), axis=0)
    params = join_parts(dot_nn(table, kinds), 8, 3)
    par_ref[...] = params
    data_ref[0:3, :] = coords_ref[...]
    data_ref[3:6, :] = params[0:3]
    data_ref[6:8, :] = params[6:8]
    head = data_ref[...]
    hist = jnp.concatenate([step_ref[...].reshape(-1, atoms), diff_ref[...].reshape(-1, atoms)], axis=0)
    rows = hist.shape[0]
    left = jnp.concatenate(split_parts(head, 3) + split_parts(hist, 2), axis=0)
    send = reordered_send(send_ref[...], sizes)
    total = None
    chunk = 256
    for first in range(0, atoms, chunk):
        part = dot_nn(left[:, first : first + chunk], send_one_hot(send, first, chunk))
        total = part if total is None else total + part
    out_ref[0:8, :] = join_parts(total[0:24], 8, 3)
    out_ref[8 : 8 + rows, :] = join_parts(total[24:], rows, 2)


def spread_rows(rows6, lanes):
    keep = (iota((8, lanes), 1) & 7) == iota((8, lanes), 0)
    return jnp.concatenate(
        [jnp.where(keep, jnp.broadcast_to(row, (8, lanes)), 0.0) for row in rows6], axis=0
    )


def cluster_map(atoms, clusters):
    return one_hot((iota((atoms, clusters), 0) >> 3) == iota((atoms, clusters), 1))


def to_clusters(rows6, lanes, clusters):
    spread = spread_rows(rows6, lanes)
    left = jnp.concatenate(split_parts(spread, 3), axis=0)
    return join_parts(dot_nn(left, cluster_map(lanes, clusters)), spread.shape[0], 3)


def to_atoms(tiles, lanes):
    clusters = tiles.shape[1]
    spread = one_hot((iota((clusters, lanes), 1) >> 3) == iota((clusters, lanes), 0))
    wide = dot_nn(jnp.concatenate(split_parts(tiles, 3), axis=0), spread)
    wide = join_parts(wide, tiles.shape[0], 3)
    keep = (iota((8, lanes), 1) & 7) == iota((8, lanes), 0)
    rows = []
    for comp in range(tiles.shape[0] // 8):
        slab = wide[comp * 8 : (comp + 1) * 8]
        rows.append(jnp.sum(jnp.where(keep, slab, 0.0), axis=0, keepdims=True))
    return rows


def lane_sum(value):
    return jnp.sum(value, axis=1, keepdims=True)


def local_kernel(coords_ref, par_ref, neigh_ref, step_ref, diff_ref, tiles_ref, other_ref, gram_ref):
    atoms = coords_ref.shape[1]
    clusters = atoms // 8
    slots = neigh_ref.shape[0]
    rows6 = [coords_ref[c : c + 1, :] for c in range(3)] + [par_ref[c : c + 1, :] for c in range(3)]
    tiles = to_clusters(rows6, atoms, clusters)
    tiles_ref[...] = tiles
    left = jnp.concatenate(split_parts(tiles, 3), axis=0)
    rows = tiles.shape[0]
    for slot in range(slots):
        select = one_hot(iota((clusters, clusters), 0) == neigh_ref[slot : slot + 1, :])
        other_ref[:, slot * clusters : (slot + 1) * clusters] = join_parts(dot_nn(left, select), rows, 3)
    memory = step_ref.shape[1]
    lane = iota((memory, 128), 1)
    sub = iota((memory, 128), 0)
    placed = jnp.zeros((memory, 128), f32)
    for j in range(memory):
        sy = None
        yy = None
        for comp in range(3):
            row = jnp.broadcast_to(diff_ref[comp, j : j + 1, :], (memory, atoms))
            one = step_ref[comp] * row
            two = diff_ref[comp] * row
            sy = one if sy is None else sy + one
            yy = two if yy is None else yy + two
        placed = placed + jnp.where(lane == sub * memory + j, lane_sum(sy), 0.0)
        placed = placed + jnp.where(lane == memory * memory + sub * memory + j, lane_sum(yy), 0.0)
    gram_ref[...] = placed


def remapped(neigh, clusters, sizes):
    face, edge, corner = (size // 8 for size in sizes)
    edge_first = clusters + 2 * face
    shift = jnp.where(
        neigh >= edge_first + edge + face,
        0,
        jnp.where(neigh >= edge_first + edge, -edge, jnp.where(neigh >= edge_first, face, 0)),
    )
    return neigh + shift


def linear_device(offset):
    total = 0
    for axis, step in zip(AXES, offset):
        count = lax.axis_size(axis)
        total = total * count + (lax.axis_index(axis) + step + count) % count
    return total


def code_bits(code):
    return code // 4, code // 2 % 2, code % 2


def pair_kernel(
    sizes, tiles_ref, other_ref, gram_ref, pz_ref, py_ref, px_ref, neigh_ref, live_ref,
    coords_ref, anchor_ref, step_ref, diff_ref,
    chunk_ref, grad_ref,
    select_ref, gather_ref, push_ref,
):
    face, edge, corner = sizes
    atoms = coords_ref.shape[1]
    clusters = atoms // 8
    slots = neigh_ref.shape[0]
    faces, edges = slab_order(sizes)
    lanes = faces + 128
    halo_clusters = 128
    memory = step_ref.shape[1]

    edge_lane = iota((pz_ref.shape[0], 128), 1)
    edge_slab = jnp.where(edge_lane < edge, py_ref[:, face : face + 128], px_ref[:, face : face + 128])
    halo = jnp.concatenate([pz_ref[:, :face], py_ref[:, :face], px_ref[:, :face], edge_slab], axis=1)
    lane = iota((1, lanes), 1)
    in_x = (lane >= 2 * face) & ((lane < faces) | (lane >= faces + edge))
    in_y = ((lane >= face) & (lane < 2 * face)) | ((lane >= faces) & (lane < faces + edge)) | (lane >= faces + 2 * edge)
    in_z = (lane < face) | ((lane >= faces) & (lane < faces + 2 * edge)) | (lane >= faces + 3 * edge)
    rows6 = [halo[c : c + 1] for c in range(6)]
    for c, inside in enumerate((in_x, in_y, in_z)):
        rows6[c] = rows6[c] + jnp.where(inside, domain_side, 0.0)
    rows6 = [jnp.where(lane < faces + edges, row, 0.0) for row in rows6]
    halo_tiles = to_clusters(rows6, lanes, halo_clusters)
    left = jnp.concatenate(split_parts(halo_tiles, 3), axis=0)
    rows = halo_tiles.shape[0]

    neigh = remapped(neigh_ref[...], clusters, sizes)
    for slot in range(slots):
        cols = slice(slot * clusters, (slot + 1) * clusters)
        row = neigh[slot : slot + 1, :]
        select_ref[:, cols] = one_hot(iota((clusters + halo_clusters, clusters), 0) == row)
        far = dot_nn(left, select_ref[clusters:, cols])
        gather_ref[:, cols] = other_ref[:, cols] + join_parts(far, rows, 3)

    rank = iota((8, clusters), 0)
    home_id = iota((8, clusters), 1)
    live = jnp.broadcast_to(live_ref[...], (8, clusters))
    full = []
    half = []
    for slot in range(slots):
        on = jnp.where(live > slot, 1.0, 0.0)
        full.append(on)
        half.append(jnp.where(neigh[slot : slot + 1, :] == home_id, 0.0, on))

    energy = jnp.zeros((8, clusters), f32)
    home_rows = [[None] * 8 for _ in range(3)]
    for p in range(8):
        home = [jnp.broadcast_to(tiles_ref[c * 8 + p : c * 8 + p + 1, :], (8, clusters)) for c in range(6)]
        upper = rank > p
        sums = [jnp.zeros((8, clusters), f32) for _ in range(3)]
        for slot in range(slots):
            cols = slice(slot * clusters, (slot + 1) * clusters)
            other = [gather_ref[c * 8 : (c + 1) * 8, cols] for c in range(6)]
            offset = [home[c] - other[c] for c in range(3)]
            dist_sq = offset[0] * offset[0] + offset[1] * offset[1] + offset[2] * offset[2]
            root = lax.rsqrt(1.0 + dist_sq)
            inverse = root * root
            repulse = home[3] * other[3] * inverse
            attract = home[4] * other[4]
            coulomb = home[5] * other[5] * root
            weight = jnp.where(upper, full[slot], half[slot])
            energy = energy + weight * (inverse * (repulse - attract) + coulomb)
            factor = weight * inverse * (inverse * (4.0 * repulse - 2.0 * attract) + coulomb)
            for c in range(3):
                term = factor * offset[c]
                sums[c] = sums[c] + term
                place = (slice(c * 8, (c + 1) * 8), cols)
                push_ref[place] = term if p == 0 else push_ref[place] + term
        for c in range(3):
            home_rows[c][p] = jnp.sum(sums[c], axis=0, keepdims=True)
    home_grad = jnp.concatenate([home_rows[c][p] for c in range(3) for p in range(8)], axis=0)
    back = jnp.concatenate(split_parts(push_ref[...], 2), axis=0)
    tile_grad = join_parts(dot_nt(back, select_ref[...]), 24, 2)
    own = to_atoms(tile_grad[:, :clusters] - home_grad, atoms)
    returned = to_atoms(tile_grad[:, clusters:], lanes)

    step_dots = jnp.zeros((memory, atoms), f32)
    diff_dots = jnp.zeros((memory, atoms), f32)
    far_step = jnp.zeros((memory, lanes), f32)
    far_diff = jnp.zeros((memory, lanes), f32)
    moved = jnp.zeros((1, atoms), f32)
    slab_lane = iota((memory, lanes), 1)
    for c in range(3):
        displacement = coords_ref[c : c + 1, :] - anchor_ref[c : c + 1, :]
        moved = moved + displacement * displacement
        grad = own[c] + displacement
        grad_ref[c : c + 1, :] = grad
        wide = jnp.broadcast_to(grad, (memory, atoms))
        step_dots = step_dots + step_ref[c] * wide
        diff_dots = diff_dots + diff_ref[c] * wide
        wide = jnp.broadcast_to(returned[c], (memory, lanes))
        far_step = far_step + halo[8 + c * memory : 8 + (c + 1) * memory] * wide
        far_diff = far_diff + halo[8 + (3 + c) * memory : 8 + (4 + c) * memory] * wide
    used = slab_lane < faces + edges
    step_sum = lane_sum(step_dots) + lane_sum(jnp.where(used, far_step, 0.0))
    diff_sum = lane_sum(diff_dots) + lane_sum(jnp.where(used, far_diff, 0.0))
    energy_sum = lane_sum(jnp.sum(energy, axis=0, keepdims=True)) + 0.5 * lane_sum(moved)
    sub = iota((memory, 128), 0)
    lane = iota((memory, 128), 1)
    dots = jnp.where(lane == sub, step_sum, 0.0) + jnp.where(lane == sub + memory, diff_sum, 0.0)
    dots = jnp.sum(dots, axis=0, keepdims=True)
    dots = dots + jnp.where(iota((1, 128), 1) == 2 * memory, energy_sum, 0.0)
    gram = jnp.sum(gram_ref[...], axis=0, keepdims=True)
    sub8 = iota((8, 128), 0)
    common = jnp.where(sub8 == 6, dots, jnp.where(sub8 == 7, gram, 0.0))
    for device in range(chunk_ref.shape[0]):
        chunk_ref[device] = common
    for code in range(1, 8):
        target = linear_device(code_bits(code))
        start = {1: 0, 2: face, 4: 2 * face}.get(code, faces)
        pieces = [returned[c][:, start : start + 128] for c in range(3)]
        if code in (1, 2, 4):
            pieces += [returned[c][:, start + 128 : start + 256] for c in range(3)]
        chunk_ref[target, 0 : len(pieces), :] = jnp.concatenate(pieces, axis=0)


def finish_kernel(sizes, atoms_total, recv_ref, send_ref, grad_ref, coords_ref, step_ref, diff_ref, new_ref, energy_ref):
    face, edge, corner = sizes
    faces, edges = slab_order(sizes)
    atoms = coords_ref.shape[1]
    memory = step_ref.shape[1]
    devices = recv_ref.shape[0]
    total = recv_ref[0]
    for device in range(1, devices):
        total = total + recv_ref[device]
    dots = jnp.broadcast_to(total[6:7, :], (memory, 128))
    gram = jnp.broadcast_to(total[7:8, :], (memory, 128))
    sub = iota((memory, 128), 0)
    lane = iota((memory, 128), 1)

    def pick(row, where):
        return jnp.broadcast_to(lane_sum(jnp.where(where, row, 0.0)), (memory, 128))

    def at(value, m):
        return jnp.broadcast_to(value[m : m + 1, :], (memory, 128))

    step_dots = pick(dots, lane == sub)
    diff_dots = pick(dots, lane == sub + memory)
    energy_ref[...] = lane_sum(jnp.where(iota((1, 128), 1) == 2 * memory, total[6:7, :], 0.0)) / atoms_total
    sy_col = [pick(gram, lane == sub * memory + j) for j in range(memory)]
    sy_row = [pick(gram, lane == j * memory + sub) for j in range(memory)]
    yy_col = [pick(gram, lane == memory * memory + sub * memory + j) for j in range(memory)]
    diagonal = pick(gram, lane == sub * (memory + 1))
    rho = 1.0 / diagonal
    last = memory - 1
    scaling = at(diagonal, last) / at(yy_col[last], last)
    left = step_dots
    alpha = jnp.zeros((memory, 128), f32)
    folded = diff_dots
    for m in reversed(range(memory)):
        value = at(left * rho, m)
        alpha = jnp.where(sub == m, value, alpha)
        left = left - value * sy_col[m]
        folded = folded - value * yy_col[m]
    left = diagonal * alpha - scaling * folded
    coef = jnp.zeros((memory, 128), f32)
    for m in range(memory):
        value = at(left * rho, m)
        coef = jnp.where(sub == m, value, coef)
        left = left - value * sy_row[m]
    diff_coef = -scaling * alpha

    blocks = {code: recv_ref[linear_device(tuple(-bit for bit in code_bits(code)))] for code in range(1, 8)}
    edge_lane = iota((8, 128), 1)
    tail = jnp.where(
        edge_lane < edge,
        blocks[3],
        jnp.where(edge_lane < 2 * edge, blocks[5], jnp.where(edge_lane < 3 * edge, blocks[6], blocks[7])),
    )
    tail = jnp.where(edge_lane < edges, tail, 0.0)
    pieces = []
    for code in (1, 2, 4):
        pieces += [blocks[code][0:3], blocks[code][3:6]]
    pieces.append(tail[0:3])
    returned = jnp.concatenate([jnp.concatenate(pieces, axis=1), jnp.zeros((5, faces + 128), f32)], axis=0)
    back = jnp.concatenate(split_parts(returned, 2), axis=0)
    send = reordered_send(send_ref[...], sizes)
    send = jnp.where(iota(send.shape, 1) < faces + edges, send, -1)
    added = []
    chunk = 256
    for first in range(0, atoms, chunk):
        added.append(join_parts(dot_nt(back, send_one_hot(send, first, chunk)), 8, 2))
    added = jnp.concatenate(added, axis=1)
    widen = atoms // 128
    for c in range(3):
        grad = grad_ref[c : c + 1, :] + added[c : c + 1, :]
        mixed = jnp.tile(coef, (1, widen)) * step_ref[c] + jnp.tile(diff_coef, (1, widen)) * diff_ref[c]
        direction = jnp.tile(scaling[0:1], (1, widen)) * grad + jnp.sum(mixed, axis=0, keepdims=True)
        new_ref[c : c + 1, :] = coords_ref[c : c + 1, :] - step_length * direction


def call(kernel, outs, scratch, *args):
    vmem = pl.BlockSpec(memory_space=pltpu.VMEM)
    return pl.pallas_call(
        kernel,
        out_shape=[jax.ShapeDtypeStruct(shape, dtype) for shape, dtype in outs],
        in_specs=[vmem] * len(args),
        out_specs=[vmem] * len(outs),
        scratch_shapes=scratch,
    )(*args)


def on_device(
    coords,
    anchor,
    atom_types,
    halo_send,
    neighbours,
    live_counts,
    rep_coef,
    disp_coef,
    charge,
    step_history,
    grad_history,
):
    atoms = coords.shape[1]
    clusters = atoms // 8
    memory = step_history.shape[0]
    sizes = export_sizes(atoms)
    face, edge, corner = sizes
    faces, edges = slab_order(sizes)
    lanes = faces + 128
    slots = neighbours.shape[1]
    devices = lax.axis_size("gx") * lax.axis_size("gy") * lax.axis_size("gz")
    assert edges <= 128 and face == 256 and 2 * memory * memory == 128
    steps = step_history.transpose(1, 0, 2)
    diffs = grad_history.transpose(1, 0, 2)
    neigh = neighbours.T
    send = jnp.pad(halo_send, (0, lanes - halo_send.shape[0]), constant_values=-1)[None]
    live = live_counts[None]
    rows = 8 + 6 * memory

    exported, params = call(
        functools.partial(export_kernel, sizes),
        [((rows, lanes), f32), ((8, atoms), f32)],
        [pltpu.VMEM((8, atoms), f32)],
        send, coords, atom_types[None], rep_coef[None], disp_coef[None], charge[None], steps, diffs,
    )
    own_edges = exported[:, faces:]
    edge_lane = lax.broadcasted_iota(i32, own_edges.shape, 1)
    sixes = (edge_lane >= 2 * edge) & (edge_lane < 3 * edge)
    fives = (edge_lane >= edge) & (edge_lane < 2 * edge)
    payload = jnp.concatenate([exported[:, :face], own_edges], axis=1)
    pz = shifted(payload, "gz", -1)
    tiles, other, gram = call(
        local_kernel,
        [((48, clusters), f32), ((48, slots * clusters), f32), ((memory, 128), f32)],
        [],
        coords, params, neigh, steps, diffs,
    )
    payload = jnp.concatenate(
        [exported[:, face : 2 * face], jnp.where(sixes, own_edges, pz[:, face:])], axis=1
    )
    py = shifted(payload, "gy", -1)
    payload = jnp.concatenate(
        [exported[:, 2 * face : faces], jnp.where(fives, pz[:, face:], py[:, face:])], axis=1
    )
    px = shifted(payload, "gx", -1)
    chunks, grad = call(
        functools.partial(pair_kernel, sizes),
        [((devices, 8, 128), f32), ((3, atoms), f32)],
        [
            pltpu.VMEM((clusters + 128, slots * clusters), bf16),
            pltpu.VMEM((48, slots * clusters), f32),
            pltpu.VMEM((24, slots * clusters), f32),
        ],
        tiles, other, gram, pz, py, px, neigh, live, coords, anchor, steps, diffs,
    )
    received = lax.all_to_all(chunks, AXES, 0, 0, tiled=True)
    new_coords, energy = call(
        functools.partial(finish_kernel, sizes, atoms * devices),
        [((3, atoms), f32), ((1, 1), f32)],
        [],
        received, send, grad, coords, steps, diffs,
    )
    return (new_coords, energy[0, 0])


def solution(mesh):
    placed = (
        P(None, AXES),
        P(None, AXES),
        P(AXES),
        P(AXES),
        P(AXES, None),
        P(AXES),
        P(),
        P(),
        P(),
        P(None, None, AXES),
        P(None, None, AXES),
    )
    return jax.shard_map(
        on_device,
        mesh=mesh,
        in_specs=placed,
        out_specs=(P(None, AXES), P()),
        check_vma=False,
    )
```

time: 140 us -> 45 us (0.32)
  other arithmetic: 26.8 us -> 0.8 us
  blocking collectives: 37.5 us -> 13.1 us
  local copies, waits for them, and re-layouts: 25.8 us -> 4.16 us
  between operations: 20.9 us -> 0.66 us
  Pallas kernels: 0 us -> 12.5 us
  matrix products: 7.65 us -> 0 us
  waiting for transfers between devices: 10 us -> 5.75 us
  starting transfers between devices: 9.5 us -> 7.65 us
    psum x1 -> x0, blocking collectives: 37.5 us -> none  [on_device(): lax.psum((jnp.dot(history, history.T, precision=highest), grad_dots_local...]
    reduce_sum x21 -> x0, other arithmetic: 14.8 us -> none  [the longest x8 5.12 us: two_loop(): jnp.sum(gram_full[1 + memory + hist_id] * coeffs)]
    all_to_all x0 -> x1, blocking collectives: none -> 13.1 us  [on_device(): received = lax.all_to_all(chunks, AXES, 0, 0, tiled=True)]
    pallas_call x0 -> x4, Pallas kernels: none -> 12.5 us  [call(): pl.pallas_call(kernel, out_shape=[jax.ShapeDtypeStruct(shape, dtype) for...]
    dot_general x6 -> x0, matrix products: 7.65 us -> none  [the longest x1 2.95 us: one_block(): jnp.einsum('cak,kj->caj', other_grad, selector, precision=highest)]
    scatter-add x1 -> x0, other arithmetic: 6.44 us -> none  [on_device(): gradient = gradient.at[:, halo_send].add(returned)]
    ppermute x6 -> x3, waiting for transfers between devices: 10 us -> 5.75 us  [shifted(): return lax.ppermute(value, axis, pairs)]
    reshape x9 -> x0, local copies, waits for them, and re-layouts: 4.24 us -> none  [the longest x1 2.67 us: one_block(): jnp.sum(push_term, axis=2).reshape(3, 8, block_rows, list_width).sum(axis=3)]
  transfers between devices with their start and end apart: 6 -> 3, of which waited for: 6 -> 2; matrix products, arithmetic and copies ran while one was open for 3% -> 0% of each run, Pallas kernels for 0% -> 6%
where the time goes in v1:
time: 45 us; the launch traced here: 44.5 us
  blocking collectives  13.1 us (29%)
  Pallas kernels  12.5 us (28%)
  starting transfers between devices  7.65 us (17%)
  waiting for transfers between devices  5.75 us (13%)
  local copies, waits for them, and re-layouts  4.16 us (9%)
  other arithmetic  0.8 us (2%)
  between operations  0.66 us (1%)
    all_to_all x1, blocking collectives, on_device(): received = lax.all_to_all(chunks, AXES, 0, 0, tiled=True)  13.1 us
    pallas_call x4, Pallas kernels, call(): pl.pallas_call(kernel, out_shape=[jax.ShapeDtypeStruct(shape, dtype) for...  12.5 us
    ppermute x3, starting transfers between devices, shifted(): return lax.ppermute(value, axis, pairs)  7.65 us
    ppermute x3, waiting for transfers between devices, shifted(): return lax.ppermute(value, axis, pairs)  5.75 us
    unnamed x6, local copies, waits for them, and re-layouts  1.26 us
  transfers between devices with their start and end apart: 3, of which 2 were waited for; matrix products, arithmetic and copies ran while one was open for 0% of the time, Pallas kernels for 6%

profile of v1, /device:TPU:0, one launch (start us, length us, event | category | flops | bytes accessed | tf_op | source)
XLA Modules:
  0.0 44.5 jit_solution(1634705616138627351)
XLA Ops:
  0.6 0.7 %pad.4 = s32[896]{0:T(1024)S(1)} pad(s32[872]{0:T(1024)} %param.14, s32[]{:T(128)} %constant.0.clone.1), padding=0_24 | pad | bytes 7076 | tf_op jit(solution)/shard_map/jit(_pad)/pad | solution.py:428
  1.3 0.6 %broadcast_in_dim.18.send_ref = s32[1,896]{1,0:T(1,128)} reshape(s32[896]{0:T(1024)S(1)} %pad.4) | data formatting | bytes 7168 | tf_op jit(solution)/shard_map/broadcast_in_dim | solution.py:428
  1.9 2.7 %shard_map.122 = (f32[56,896]{1,0:T(8,128)}, f32[8,2048]{1,0:T(8,128)}) custom-call(s32[1,896]{1,0:T(1,128)} %broadcast_in_dim.18.send_ref, f32[3,2048]{1,0:T(4,128)} %coords_ref.7, s32[1,2048]{1,0:T(1,128)} %bitcast.19, f32[1,64]{1,0:T(1,128)} %bitcast.21, f32[1,64]{1,0:T(1,128)} %bitcast.22, f32[1,64]{1,0:T(1,128)} %bitcast.23, f32[3,8,2048]{2,1,0:T(8,128)} %bitcast.9, ...), custom_call_target="tpu_custom_call" | custom-call | tf_op jit(solution)/shard_map/pallas_call | solution.py:393
  4.6 0.8 %slice.20 = f32[56,128]{1,0:T(8,128)S(1)} slice(f32[56,896]{1,0:T(8,128)} %get-tuple-element.15), slice={[0:56], [768:896]} | slice | bytes 57344 | tf_op jit(solution)/shard_map/slice | solution.py:438
  5.3 0.9 %fusion = (f32[56,256]{1,0:T(8,128)S(1)}, f32[56,256]{1,0:T(8,128)S(1)}, f32[56,256]{1,0:T(8,128)S(1)}) fusion(f32[56,896]{1,0:T(8,128)} %get-tuple-element.15), kind=kLoop, calls=%fused_computation.7 | loop fusion | bytes 344064 | tf_op jit(solution)/shard_map/slice | solution.py:455
  6.2 2.5 %collective-permute-start = (f32[56,384]{1,0:T(8,128)S(1)}, f32[56,384]{1,0:T(8,128)S(1)}, u32[]{:S(2)}, u32[]{:S(2)}) collective-permute-start(f32[56,384]{1,0:T(8,128)S(1)} %pad_maximum_fusion), channel_id=1, source_target_pairs={{0,3},{1,0},{2,1},{3,2},{4,7},{5,4},{6,5},{7,6},{8,11},{9,8},{10,9... | collective-permute-start | bytes 258056 | tf_op jit(solution)/shard_map/ppermute | solution.py:28
  8.7 2.1 %collective-permute-done.pz_ref = f32[56,384]{1,0:T(8,128)S(1)} collective-permute-done((f32[56,384]{1,0:T(8,128)S(1)}, f32[56,384]{1,0:T(8,128)S(1)}, u32[]{:S(2)}, u32[]{:S(2)}) %collective-permute-start) | collective-permute-done | bytes 86048 | tf_op jit(solution)/shard_map/ppermute | solution.py:28
  10.8 0.0 copy-start
  10.8 0.8 %slice_select_fusion.1 = f32[56,128]{1,0:T(8,128)S(1)} fusion(f32[56,384]{1,0:T(8,128)S(1)} %collective-permute-done.pz_ref, pred[128]{0:T(512)(128)(4,1)S(1)} %compare_and_fusion.1, f32[56,896]{1,0:T(8,128)} %get-tuple-element.15), kind=kLoop, calls=%fused_computation.4 | loop fusion | flops 7168 | bytes 86144 | tf_op jit(solution)/shard_map/jit(_where)/select_n | solution.py:451
  11.5 1.6 %collective-permute-start.1 = (f32[56,384]{1,0:T(8,128)S(1)}, f32[56,384]{1,0:T(8,128)S(1)}, u32[]{:S(2)}, u32[]{:S(2)}) collective-permute-start(f32[56,384]{1,0:T(8,128)S(1)} %pad_maximum_fusion.1), channel_id=1, source_target_pairs={{0,4},{4,0},{1,5},{5,1},{2,6},{6,2},{3,7},{7,3},{8,12},{12,8},{9,1... | collective-permute-start | bytes 258056 | tf_op jit(solution)/shard_map/ppermute | solution.py:28
  13.1 3.7 %collective-permute-done.1.py_ref = f32[56,384]{1,0:T(8,128)S(1)} collective-permute-done((f32[56,384]{1,0:T(8,128)S(1)}, f32[56,384]{1,0:T(8,128)S(1)}, u32[]{:S(2)}, u32[]{:S(2)}) %collective-permute-start.1) | collective-permute-done | bytes 86048 | tf_op jit(solution)/shard_map/ppermute | solution.py:28
  16.8 0.0 copy-done
  16.8 0.0 copy-start.1
  16.8 0.6 %copy-done.1 = f32[56,384]{1,0:T(8,128)} copy-done((f32[56,384]{1,0:T(8,128)}, f32[56,384]{1,0:T(8,128)S(1)}, u32[]{:S(2)}) %copy-start.1) | copy-done | bytes 86040
  17.4 3.6 %collective-permute-start.2 = (f32[56,384]{1,0:T(8,128)S(1)}, f32[56,384]{1,0:T(8,128)S(1)}, u32[]{:S(2)}, u32[]{:S(2)}) collective-permute-start(f32[56,384]{1,0:T(8,128)S(1)} %pad_maximum_fusion.2), channel_id=1, source_target_pairs={{0,24},{8,0},{16,8},{24,16},{1,25},{9,1},{17,9},{25,17},{2,26},{10... | collective-permute-start | bytes 258056 | tf_op jit(solution)/shard_map/ppermute | solution.py:28
  21.0 2.9 %shard_map.123 = (f32[48,256]{1,0:T(8,128)}, f32[48,2048]{1,0:T(8,128)}, f32[8,128]{1,0:T(8,128)}) custom-call(f32[3,2048]{1,0:T(4,128)} %coords_ref.7, f32[8,2048]{1,0:T(8,128)} %get-tuple-element.11.par_ref, s32[8,256]{1,0:T(8,128)} %bitcast.17, f32[3,8,2048]{2,1,0:T(8,128)} %bitcast.10, f32[3,8,2048]{2,1,0:T(8,128)} %bitcast.14), custom_call_target="tpu_custom_call" | custom-call | tf_op jit(solution)/shard_map/pallas_call | solution.py:393
  23.9 0.0 collective-permute-done.2.px_ref
  23.9 0.0 copy-start.2
  23.9 0.6 %copy-done.2 = f32[56,384]{1,0:T(8,128)} copy-done((f32[56,384]{1,0:T(8,128)}, f32[56,384]{1,0:T(8,128)S(1)}, u32[]{:S(2)}) %copy-start.2) | copy-done | bytes 86040
  24.5 4.1 %shard_map.124 = (f32[32,8,128]{2,1,0:T(8,128)}, f32[3,2048]{1,0:T(4,128)}) custom-call(f32[48,256]{1,0:T(8,128)} %get-tuple-element.12.tiles_ref, f32[48,2048]{1,0:T(8,128)} %get-tuple-element.13.other_ref, f32[8,128]{1,0:T(8,128)} %get-tuple-element.14.gram_ref, f32[56,384]{1,0:T(8,128)} %copy-done, f32[56,384]{1,0:T(8,128)} %copy-done.1, ...), custom_call_target="tpu_custom_call" | custom-call | tf_op jit(solution)/shard_map/pallas_call | solution.py:393
  28.6 13.1 %all_to_all.5.recv_ref = f32[32,8,128]{2,1,0:T(8,128)} all-to-all(f32[32,8,128]{2,1,0:T(8,128)} %get-tuple-element.16), channel_id=1, replica_groups=mesh['gx'=4,'gy'=2,'gz'=4] {'gx','gy','gz'}, dimensions={0} | all-to-all | bytes 262144 | tf_op jit(solution)/shard_map/all_to_all | solution.py:468
  41.7 2.8 %shard_map.125 = (f32[3,2048]{1,0:T(4,128)}, f32[1,1]{1,0:T(1,128)}) custom-call(f32[32,8,128]{2,1,0:T(8,128)} %all_to_all.5.recv_ref, s32[1,896]{1,0:T(1,128)} %broadcast_in_dim.18.send_ref, f32[3,2048]{1,0:T(4,128)} %get-tuple-element.17.grad_ref, f32[3,2048]{1,0:T(4,128)} %coords_ref.7, f32[3,8,2048]{2,1,0:T(8,128)} %bitcast.12, f32[3,8,2048]{2,1,0:T(8,128)} %bitcast.16), custom_call_target="tpu_custom_call" | custom-call | tf_op jit(solution)/shard_map/pallas_call | solution.py:393
  (6 shorter events, 0.0 us)
Async XLA Ops:
  6.2 4.6 %collective-permute-start = (f32[56,384]{1,0:T(8,128)S(1)}, f32[56,384]{1,0:T(8,128)S(1)}, u32[]{:S(2)}, u32[]{:S(2)}) collective-permute-start(f32[56,384]{1,0:T(8,128)S(1)} %pad_maximum_fusion), channel_id=1, source_target_pairs={{0,3},{1,0},{2,1},{3,2},{4,7},{5,4},{6,5},{7,6},{8,11},{9,8},{10,9... | collective-permute-start | bytes 258056 | tf_op jit(solution)/shard_map/ppermute | solution.py:28
  10.8 6.0 %copy-start = (f32[56,384]{1,0:T(8,128)}, f32[56,384]{1,0:T(8,128)S(1)}, u32[]{:S(2)}) copy-start(f32[56,384]{1,0:T(8,128)S(1)} %collective-permute-done.pz_ref) | copy-start | bytes 258052
  11.5 5.2 %collective-permute-start.1 = (f32[56,384]{1,0:T(8,128)S(1)}, f32[56,384]{1,0:T(8,128)S(1)}, u32[]{:S(2)}, u32[]{:S(2)}) collective-permute-start(f32[56,384]{1,0:T(8,128)S(1)} %pad_maximum_fusion.1), channel_id=1, source_target_pairs={{0,4},{4,0},{1,5},{5,1},{2,6},{6,2},{3,7},{7,3},{8,12},{12,8},{9,1... | collective-permute-start | bytes 258056 | tf_op jit(solution)/shard_map/ppermute | solution.py:28
  16.8 0.6 %copy-start.1 = (f32[56,384]{1,0:T(8,128)}, f32[56,384]{1,0:T(8,128)S(1)}, u32[]{:S(2)}) copy-start(f32[56,384]{1,0:T(8,128)S(1)} %collective-permute-done.1.py_ref) | copy-start | bytes 258052
  17.4 6.5 %collective-permute-start.2 = (f32[56,384]{1,0:T(8,128)S(1)}, f32[56,384]{1,0:T(8,128)S(1)}, u32[]{:S(2)}, u32[]{:S(2)}) collective-permute-start(f32[56,384]{1,0:T(8,128)S(1)} %pad_maximum_fusion.2), channel_id=1, source_target_pairs={{0,24},{8,0},{16,8},{24,16},{1,25},{9,1},{17,9},{25,17},{2,26},{10... | collective-permute-start | bytes 258056 | tf_op jit(solution)/shard_map/ppermute | solution.py:28
  23.9 0.6 %copy-start.2 = (f32[56,384]{1,0:T(8,128)}, f32[56,384]{1,0:T(8,128)S(1)}, u32[]{:S(2)}) copy-start(f32[56,384]{1,0:T(8,128)S(1)} %collective-permute-done.2.px_ref) | copy-start | bytes 258052
